TPU v7x, 32 devices: a whole 2x2x4 slice. The times are simulated.
32 devices in a mesh: groups: 2 (over y), seq: 4 (over z), head: 4 (over x, core).
Axes of the slice: x: 2, y: 2, z: 4, core: 2. Of those that a mesh axis runs over, the one named last changes fastest.
Arguments:
- tile_tokens: bfloat16 [16, 256, 1536], P(('groups', 'seq')), parts along dimension 0, may hold values from -6 to 6
- tile_gain: float32 [1536], replicated, may hold values from 0.1 to 1.9
- w_gate_up: bfloat16 [2, 1536, 4096], P(None, 'seq', 'head'), may hold values from -0.15625 to 0.15625
- w_down: bfloat16 [4096, 1536], P('head', 'seq'), may hold values from -0.09375 to 0.09375
- layer_scale: float32 [1536], replicated, may hold values from 1 to 8
- fc_gain: float32 [1536], replicated, may hold values from 0.1 to 1.9
- w_embed: bfloat16 [1536, 768], P(None, 'head'), may hold values from -0.15625 to 0.15625
- embed_bias: float32 [768], P('head'), may hold values from -3 to 3
- pre_emb: bfloat16 [2032, 768], P(('groups', 'seq'), 'head'), parts along dimension 0, may hold values from -6 to 6
- tile_order: int32 [2048], P('groups'), parts along dimension 0, may hold values from 0 to 1023, as said below
- valid_count: int32 [2], P('groups'), parts along dimension 0, may hold values from 256 to 1024
- slide_gain: float32 [768], replicated, may hold values from 0.1 to 1.9
- w_qkv: bfloat16 [3, 768, 768], P(None, None, 'head'), may hold values from -1.25 to 1.25
- sub_gain: float32 [768], P('head'), may hold values from 0.1 to 1.9
- w_out: bfloat16 [768, 768], P('head'), may hold values from -0.21875 to 0.21875
Outputs:
- mixed: float32 [2048, 768], P(('groups', 'seq'), 'head'), parts along dimension 0
There are 2 independent parts, one for each index of `groups`. A program takes and returns all parts, laid end to end along the dimension named above; an argument that names none is the same for every part. Nothing has to cross between parts.
Inputs may be any that keep to these rules, and one draw needn't show every extreme that they name: `tile_order`: A permutation of 0 to 1023. For every block of 256 positions (d * 256 to (d + 1) * 256 - 1) and every block of 256 stored rows, exactly 64 positions of the first take rows of the second.
All inputs are finite; a program needn't handle non-finite values.
Results may differ from a plain program's by a relative error of at most 0.0046.
Values may be sent and summed in bfloat16 or wider, within the bound.
A program may use at most 64 MiB of HBM per device.

v0:
```python
import math
import jax
import jax.numpy as jnp
from jax import lax
from jax.sharding import PartitionSpec as P

DS = 768
HEAD_DIM = 48
SPAN0 = 1024
SPAN1 = 4096
DILATION_SECOND = 4
DILATION_THIRD = 16
layer_eps = 1e-05
masked_score = -1e30


def from_partner(value, axis, bit):
    mask = 2**bit
    pairs = [(source, source ^ mask) for source in range(lax.axis_size(axis))]
    return lax.ppermute(value, axis, pairs)


def normalize(values, gain):
    centered = values - jnp.mean(values, axis=-1, keepdims=True)
    variance = jnp.mean(centered * centered, axis=-1, keepdims=True)
    return centered * lax.rsqrt(variance + layer_eps) * gain


def select_rows(stacked, dilation, offsets):
    group_count, row_count, row_width = stacked.shape
    head_count = offsets.shape[0]
    arranged = stacked.reshape(
        group_count, row_count // dilation, dilation, head_count, row_width // head_count
    )
    choose = jnp.arange(dilation, dtype=jnp.int32)[:, None] == offsets[None, :]
    chosen = jnp.sum(
        jnp.where(choose[None, None, :, :, None], arranged, jnp.zeros((), stacked.dtype)), axis=2
    )
    return chosen.reshape(group_count, row_count // dilation, row_width)


def scatter_rows(attended, log_mass, dilation, offsets):
    query_count, head_count, head_size = attended.shape
    choose = jnp.arange(dilation, dtype=jnp.int32)[:, None] == offsets[None, :]
    spread_out = jnp.where(choose[None, :, :, None], attended[:, None, :, :], 0.0).reshape(
        query_count * dilation, head_count, head_size
    )
    spread_mass = jnp.where(choose[None, :, :], log_mass[:, None, :], masked_score).reshape(
        query_count * dilation, head_count
    )
    selected = jnp.broadcast_to(choose[None, :, :], (query_count, dilation, head_count)).reshape(
        query_count * dilation, head_count
    )
    return (spread_out, spread_mass, selected)


def attend(query_rows, key_rows, value_rows, positions, valid_limit, head_count):
    head_size = query_rows.shape[1] // head_count
    query_heads = query_rows.reshape(query_rows.shape[0], head_count, head_size)
    key_heads = key_rows.reshape(key_rows.shape[0], head_count, head_size)
    value_heads = value_rows.reshape(value_rows.shape[0], head_count, head_size)
    scores = jnp.einsum(
        "qhe,khe->hqk", query_heads, key_heads, preferred_element_type=jnp.float32
    ) / math.sqrt(head_size)
    scores = jnp.where((positions < valid_limit)[:, None, :], scores, masked_score)
    highest = jnp.max(scores, axis=-1, keepdims=True)
    exponent = jnp.exp(scores - highest)
    mass_sum = jnp.sum(exponent, axis=-1, keepdims=True)
    weights = (exponent / mass_sum).astype(jnp.bfloat16)
    attended = jnp.einsum("hqk,khe->qhe", weights, value_heads, preferred_element_type=jnp.float32)
    return (attended, (highest[..., 0] + jnp.log(mass_sum[..., 0])).T)


def body(
    tile_tokens,
    tile_gain,
    w_gate_up,
    w_down,
    layer_scale,
    fc_gain,
    w_embed,
    embed_bias,
    pre_emb,
    tile_order,
    valid_count,
    slide_gain,
    w_qkv,
    sub_gain,
    w_out,
):
    new_count, patch_count, tile_width = tile_tokens.shape
    token_rows = tile_tokens.reshape(new_count * patch_count, tile_width)
    normed = normalize(token_rows.astype(jnp.float32), tile_gain).astype(jnp.bfloat16)
    hidden_width = w_gate_up.shape[2]
    gate_up = jnp.einsum(
        "rk,gkf->grf",
        normed,
        lax.all_gather(w_gate_up, "seq", axis=1, tiled=True),
        preferred_element_type=jnp.float32,
    )
    hidden = (jax.nn.silu(gate_up[0]) * gate_up[1]).astype(jnp.bfloat16)
    pooled_hidden = jnp.mean(
        hidden.reshape(new_count, patch_count, hidden_width), axis=1, dtype=jnp.float32
    )
    everyone = lax.all_gather(pooled_hidden, "seq", axis=0, tiled=True)
    local_part = jnp.dot(everyone, w_down.astype(jnp.float32), precision=lax.Precision.HIGHEST)
    pooled_part = lax.all_to_all(local_part, "seq", split_axis=0, concat_axis=1, tiled=True)
    summed = lax.psum(pooled_part, "head")
    pooled = jnp.mean(tile_tokens, axis=1, dtype=jnp.float32) + layer_scale * summed
    feature = normalize(pooled, fc_gain).astype(jnp.bfloat16)
    new_rows = (jnp.dot(feature, w_embed, preferred_element_type=jnp.float32) + embed_bias).astype(
        jnp.bfloat16
    )
    stored = jnp.concatenate([new_rows, pre_emb], axis=0)
    block_rows = stored.shape[0]
    total_rows = tile_order.shape[0]
    peer_rows = block_rows // lax.axis_size("seq")
    device = lax.axis_index("seq")
    local_index = jnp.arange(block_rows, dtype=jnp.int32)
    inverse = (
        jnp.zeros((total_rows,), jnp.int32)
        .at[tile_order]
        .set(jnp.arange(total_rows, dtype=jnp.int32))
    )
    placed = lax.dynamic_slice_in_dim(inverse, device * block_rows, block_rows)
    target = placed // block_rows
    before = (target[:, None] == target[None, :]) & (placed[None, :] < placed[:, None])
    slot_index = target * peer_rows + jnp.sum(before, axis=1, dtype=jnp.int32)
    routing = (slot_index[None, :] == local_index[:, None]).astype(jnp.bfloat16)
    outgoing = jnp.dot(routing, stored, preferred_element_type=jnp.float32).astype(jnp.bfloat16)
    incoming = lax.all_to_all(outgoing, "seq", split_axis=0, concat_axis=0, tiled=True)
    wanted = lax.dynamic_slice_in_dim(tile_order, device * block_rows, block_rows)
    source = wanted // block_rows
    earlier = (source[:, None] == source[None, :]) & (local_index[None, :] < local_index[:, None])
    arrival = source * peer_rows + jnp.sum(earlier, axis=1, dtype=jnp.int32)
    own_part = jnp.take(incoming, arrival, axis=0)
    sequence = lax.all_gather(own_part, "head", axis=1, tiled=True)
    slide_normed = normalize(sequence.astype(jnp.float32), slide_gain).astype(jnp.bfloat16)
    projected_rows = jnp.einsum(
        "rd,gdc->grc", slide_normed, w_qkv, preferred_element_type=jnp.float32
    ).astype(jnp.bfloat16)
    cols_here = projected_rows.shape[2]
    head_count = cols_here // HEAD_DIM
    head_indices = lax.axis_index("head") * head_count + jnp.arange(head_count, dtype=jnp.int32)
    valid_limit = valid_count[0]
    row_index = device * block_rows + local_index
    near_devices = min(SPAN0, total_rows) // block_rows
    near_rows = projected_rows[1:]
    for bit_index in range(near_devices.bit_length() - 1):
        partner = from_partner(near_rows, "seq", bit_index)
        upper_half = device // (1 << bit_index) % 2 == 1
        near_rows = jnp.where(
            upper_half,
            jnp.concatenate([partner, near_rows], 1),
            jnp.concatenate([near_rows, partner], 1),
        )
    near_start = device // near_devices * near_devices * block_rows
    near_pos = jnp.broadcast_to(
        near_start + jnp.arange(near_rows.shape[1], dtype=jnp.int32),
        (head_count, near_rows.shape[1]),
    )
    near_out, near_mass = attend(
        projected_rows[0], near_rows[0], near_rows[1], near_pos, valid_limit, head_count
    )
    near_sel = jnp.ones((block_rows, head_count), dtype=bool)
    middle_level_offsets = head_indices % DILATION_SECOND
    middle_level = select_rows(projected_rows, DILATION_SECOND, middle_level_offsets)
    middle_devices = min(SPAN1, total_rows) // block_rows
    middle_key_value = middle_level[1:]
    every_row = lax.all_gather(middle_key_value, "seq", axis=1, tiled=True)
    group_rows = middle_devices * middle_key_value.shape[1]
    middle_key_value = lax.dynamic_slice_in_dim(
        every_row, device // middle_devices * group_rows, group_rows, 1
    )
    middle_start = device // middle_devices * middle_devices * block_rows
    middle_pos = (
        middle_start
        + middle_level_offsets[:, None]
        + DILATION_SECOND * jnp.arange(middle_key_value.shape[1], dtype=jnp.int32)[None, :]
    )
    middle_attention, middle_log_sum = attend(
        middle_level[0],
        middle_key_value[0],
        middle_key_value[1],
        middle_pos,
        valid_limit,
        head_count,
    )
    middle_output, middle_level_mass, middle_selected = scatter_rows(
        middle_attention, middle_log_sum, DILATION_SECOND, middle_level_offsets
    )
    distant_offsets = head_indices % DILATION_THIRD
    distant_local_rows = select_rows(projected_rows, DILATION_THIRD, distant_offsets)
    distant_key_value = lax.all_gather(distant_local_rows[1:], "seq", axis=1, tiled=True)
    distant_positions = (
        distant_offsets[:, None]
        + DILATION_THIRD * jnp.arange(distant_key_value.shape[1], dtype=jnp.int32)[None, :]
    )
    distant_attention, distant_log_sum = attend(
        distant_local_rows[0],
        distant_key_value[0],
        distant_key_value[1],
        distant_positions,
        valid_limit,
        head_count,
    )
    distant_output, distant_mass, distant_selected = scatter_rows(
        distant_attention, distant_log_sum, DILATION_THIRD, distant_offsets
    )
    outputs = jnp.stack([near_out, middle_output, distant_output])
    masses = jnp.stack([near_mass, middle_level_mass, distant_mass])
    selects = jnp.stack([near_sel, middle_selected, distant_selected])
    ceiling = jnp.max(masses, axis=0)
    shares = jnp.where(selects, jnp.exp(masses - ceiling), 0.0)
    combined = jnp.sum(shares[..., None] * outputs, axis=0) / jnp.sum(shares, axis=0)[..., None]
    combined = jnp.where((row_index < valid_limit)[:, None, None], combined, 0.0).reshape(
        block_rows, cols_here
    )
    row_total, row_square = lax.psum(
        (jnp.sum(combined, axis=1), jnp.sum(combined * combined, axis=1)), "head"
    )
    mean_value = row_total / DS
    mean_square = row_square / DS
    scaling = lax.rsqrt(mean_square - mean_value * mean_value + layer_eps)
    settled = ((combined - mean_value[:, None]) * scaling[:, None] * sub_gain).astype(jnp.bfloat16)
    partial_rows = jnp.dot(settled, w_out, preferred_element_type=jnp.float32)
    branch_sum = lax.psum_scatter(partial_rows, "head", scatter_dimension=1, tiled=True)
    return own_part.astype(jnp.float32) + branch_sum


def solution(mesh):
    placed = (
        P(("groups", "seq"), None, None),
        P(),
        P(None, "seq", "head"),
        P("head", "seq"),
        P(),
        P(),
        P(None, "head"),
        P("head"),
        P(("groups", "seq"), "head"),
        P("groups"),
        P("groups"),
        P(),
        P(None, None, "head"),
        P("head"),
        P("head", None),
    )
    return jax.shard_map(
        body, mesh=mesh, in_specs=placed, out_specs=P(("groups", "seq"), "head"), check_vma=False
    )
```

profile of v0, /device:TPU:0, one launch (start us, length us, event | category | flops | bytes accessed | tf_op | source)
XLA Modules:
  0.0 281.4 jit_solution(12463239555199441893)
XLA Ops:
  6.6 0.7 all-gather.3.cloned.1.call-update
  7.3 2.0 convert_reduce_fusion.1
  9.3 0.5 multiply_reduce_fusion
  10.5 4.3 %scatter_custom_fusion = s32[1024]{0:T(1024)S(1)} fusion(s32[1024]{0:T(1024)S(1)} %compare_select_fusion, s32[1024]{0:T(1024)S(1)} %iota.73, s32[]{:T(128)} %constant.151.clone.1), kind=kCustom, calls=%fused_computation.103 | custom fusion | bytes 4100 | tf_op jit(solution)/shard_map/scatter | solution.py:123
  15.0 0.2 convert_reduce_fusion.5
  15.2 0.2 convert_reduce_fusion.4
  15.6 1.7 fusion.4
  17.3 109.7 %all-gather.3.cloned.1.call-done = bf16[2,1536,1024]{2,1,0:T(8,128)(2,1)} async-done(((bf16[2,384,1024]{2,1,0:T(8,128)(2,1)}), bf16[2,1536,1024]{2,1,0:T(8,128)(2,1)}) %all-gather.3.cloned.1.call-update) | async-done | bytes 6291472 | tf_op jit(solution)/shard_map/all_gather | solution.py:98
  127.0 6.0 %convolution_bitcast_fusion = f32[2,512,1024]{2,1,0:T(8,128)S(1)} fusion(bf16[2,1536,1024]{2,1,0:T(8,128)(2,1)} %all-gather.3.cloned.1.call-done, bf16[512,1536]{1,0:T(8,128)(2,1)} %fusion.4), kind=kOutput, calls=%fused_computation.14 | convolution fusion | flops 3221225472 | bytes 12058624 | tf_op jit(solution)/shard_map/rk,gkf->grf/dot_general | solution.py:95
  133.0 0.6 fusion.51
  133.6 0.6 convert_reduce_fusion.2
  134.2 13.2 %all-gather = f32[4,2,1024]{2,1,0:T(2,128)S(1)} all-gather(f32[1,2,1024]{2,1,0:T(2,128)S(1)} %multiply_bitcast_fusion), channel_id=1, replica_groups=mesh['groups'=2,'seq'=4,'head'=4] {'seq'}, dimensions={0}, use_global_device_ids=true | all-gather | bytes 40960 | tf_op jit(solution)/shard_map/all_gather | solution.py:105
  147.5 0.4 fusion.57
  147.9 0.6 all_to_all.22
  148.5 3.3 %all-to-all-start = ((f32[4,2,384]{2,1,0:T(2,128)}), f32[4,2,384]{2,1,0:T(2,128)S(1)}, u32[]{:S(2)}, u32[]{:S(2)}) async-start(f32[4,2,384]{2,1,0:T(2,128)} %all_to_all.22), calls=%async_computation | async-start | bytes 24576 | tf_op jit(solution)/shard_map/all_to_all | solution.py:107
  151.8 5.6 %all-to-all-done = f32[4,2,384]{2,1,0:T(2,128)S(1)} async-done(((f32[4,2,384]{2,1,0:T(2,128)}), f32[4,2,384]{2,1,0:T(2,128)S(1)}, u32[]{:S(2)}, u32[]{:S(2)}) %all-to-all-start) | async-done | bytes 12320 | tf_op jit(solution)/shard_map/all_to_all | solution.py:107
  157.3 10.1 %psum.21 = f32[2,1536]{1,0:T(2,128)S(1)} all-reduce(f32[2,1536]{1,0:T(2,128)S(1)} %bitcast.134), channel_id=1, replica_groups=mesh['groups'=2,'seq'=4,'head'=4] {'head'}, use_global_device_ids=true, to_apply=%region_7.8 | all-reduce | flops 3072 | bytes 24576 | tf_op jit(solution)/shard_map/psum | solution.py:108
  167.4 0.1 fusion.50
  167.6 0.2 multiply_reduce_fusion.2
  167.8 0.3 fusion.10
  168.1 0.2 copy.70
  168.3 0.2 convolution_convert_fusion
  168.5 0.8 copy.71
  169.3 3.3 %all-to-all-start.1 = ((bf16[4,64,192]{2,1,0:T(8,128)(2,1)}), bf16[4,64,192]{2,1,0:T(8,128)(2,1)S(1)}, u32[]{:S(2)}, u32[]{:S(2)}) async-start(bf16[4,64,192]{2,1,0:T(8,128)(2,1)} %bitcast.8), calls=%async_computation.1 | async-start | bytes 262144 | tf_op jit(solution)/shard_map/all_to_all | solution.py:131
  172.8 0.1 stack.19
  173.0 0.1 broadcast_in_dim.279
  173.4 5.2 %all-to-all-done.1 = bf16[4,64,192]{2,1,0:T(8,128)(2,1)S(1)} async-done(((bf16[4,64,192]{2,1,0:T(8,128)(2,1)}), bf16[4,64,192]{2,1,0:T(8,128)(2,1)S(1)}, u32[]{:S(2)}, u32[]{:S(2)}) %all-to-all-start.1) | async-done | bytes 98336 | tf_op jit(solution)/shard_map/all_to_all | solution.py:131
  178.6 1.2 gather_fusion
  179.9 6.4 %all_gather.17 = bf16[256,768]{0,1:T(8,128)(2,1)S(1)} all-gather(bf16[256,192]{0,1:T(8,128)(2,1)S(1)} %broadcast_select_fusion.2), channel_id=1, replica_groups=mesh['groups'=2,'seq'=4,'head'=4] {'head'}, dimensions={1}, use_global_device_ids=true | all-gather | bytes 491520 | tf_op jit(solution)/shard_map/all_gather | solution.py:137
  186.4 0.2 fusion.13
  186.6 0.5 fusion.17
  187.2 0.2 copy.76
  187.4 0.4 reshape.504
  187.8 0.7 select_reduce_fusion.1
  188.6 0.1 copy.78
  188.7 0.1 copy.79
  188.8 14.0 %all_gather.18 = bf16[2,256,192]{2,0,1:T(2,128)(2,1)S(1)} all-gather(bf16[2,64,192]{2,0,1:T(2,128)(2,1)S(1)} %copy.79), channel_id=1, replica_groups=mesh['groups'=2,'seq'=4,'head'=4] {'seq'}, dimensions={1}, use_global_device_ids=true | all-gather | bytes 245760 | tf_op jit(solution)/shard_map/all_gather | solution.py:170
  202.9 0.4 fusion.53
  203.2 0.1 copy.80
  203.5 0.3 fusion.56
  203.8 0.2 fusion.23
  204.1 0.1 broadcast_in_dim.271
  204.2 0.1 broadcast_in_dim.280
  204.4 0.4 reshape.505
  204.8 0.6 select_reduce_fusion
  205.5 13.3 %all_gather.19 = bf16[2,64,192]{2,1,0:T(8,128)(2,1)S(1)} all-gather(bf16[2,16,192]{2,1,0:T(8,128)(2,1)S(1)} %slice.61), channel_id=1, replica_groups=mesh['groups'=2,'seq'=4,'head'=4] {'seq'}, dimensions={1}, use_global_device_ids=true | all-gather | bytes 61440 | tf_op jit(solution)/shard_map/all_gather | solution.py:194
  218.9 0.2 fusion.55
  219.2 0.2 fusion.33
  219.6 0.1 copy.84
  219.8 0.3 convolution_bitcast_fusion.1
  220.3 0.2 copy.86
  220.6 0.2 convolution_bitcast_fusion.2
  220.8 0.2 copy.88
  221.1 6.2 %collective-permute-done = bf16[2,256,192]{1,2,0:T(8,128)(2,1)S(1)} collective-permute-done((bf16[2,256,192]{1,2,0:T(8,128)(2,1)S(1)}, bf16[2,256,192]{1,2,0:T(8,128)(2,1)S(1)}, u32[]{:S(2)}, u32[]{:S(2)}) %collective-permute-start) | collective-permute-done | bytes 196640 | tf_op jit(solution)/shard_map/ppermute | solution.py:20
  227.3 0.8 collective-permute-start.1
  228.2 11.7 %collective-permute-done.1 = bf16[2,512,192]{1,2,0:T(8,128)(2,1)S(1)} collective-permute-done((bf16[2,512,192]{1,2,0:T(8,128)(2,1)S(1)}, bf16[2,512,192]{1,2,0:T(8,128)(2,1)S(1)}, u32[]{:S(2)}, u32[]{:S(2)}) %collective-permute-start.1) | collective-permute-done | bytes 393248 | tf_op jit(solution)/shard_map/ppermute | solution.py:20
  239.9 0.2 maximum_select_fusion
  240.2 0.9 fusion
  241.0 1.0 fusion.1
  242.1 1.2 fusion.8
  243.6 5.7 %all-reduce = (f32[256]{0:T(256)S(1)}, f32[256]{0:T(256)S(1)}) all-reduce(f32[256]{0:T(256)S(1)} %get-tuple-element.8, f32[256]{0:T(256)S(1)} %get-tuple-element.7), channel_id=1, replica_groups=mesh['groups'=2,'seq'=4,'head'=4] {'head'}, use_global_device_ids=true, to_apply=%region_25.26 | all-reduce | flops 512 | bytes 4096 | tf_op jit(solution)/shard_map/psum | solution.py:219
  249.4 1.2 fusion.58
  250.6 22.4 %reduce-scatter.2.cloned.1.call-done = f32[256,192]{0,1:T(8,128)} async-done(((f32[256,768]{0,1:T(8,128)}), f32[256,192]{0,1:T(8,128)}) %reduce-scatter.2.cloned.1.call-update) | async-done | bytes 196624 | tf_op jit(solution)/shard_map/reduce_scatter | solution.py:227
  273.0 1.6 convert_add_fusion
  (103 shorter events, 3.0 us)
Async XLA Ops:
  6.5 180.1 %copy-start = (bf16[3,768,192]{1,2,0:T(8,128)(2,1)S(1)}, bf16[3,768,192]{1,2,0:T(8,128)(2,1)}, u32[]{:S(2)}) copy-start(bf16[3,768,192]{1,2,0:T(8,128)(2,1)} %param.27) | copy-start | bytes 2654212
  6.5 2.7 copy-start.1
  6.5 4.0 %copy-start.7 = (s32[1024]{0:T(1024)S(1)}, s32[1024]{0:T(1024)}, u32[]{:S(2)}) copy-start(s32[1024]{0:T(1024)} %param.24) | copy-start | bytes 12292
  6.5 9.1 %copy-start.5 = (f32[1536]{0:T(1024)S(1)}, f32[1536]{0:T(1024)}, u32[]{:S(2)}) copy-start(f32[1536]{0:T(1024)} %param.16) | copy-start | bytes 18436
  6.5 120.5 %all-gather.3.cloned.1.call-start = ((), (), s32[]{:S(2)}) async-start(), calls=%async_computation.3 | async-start | bytes 7864320 | tf_op jit(solution)/shard_map/all_gather | solution.py:98
  133.6 13.9 %copy-start.3 = (bf16[1024,384]{1,0:T(8,128)(2,1)S(1)}, bf16[1024,384]{1,0:T(8,128)(2,1)}, u32[]{:S(2)}) copy-start(bf16[1024,384]{1,0:T(8,128)(2,1)} %param.18) | copy-start | bytes 2359300
  133.6 33.9 %copy-start.6 = (f32[1536]{0:T(1024)S(1)}, f32[1536]{0:T(1024)}, u32[]{:S(2)}) copy-start(f32[1536]{0:T(1024)} %param.19) | copy-start | bytes 18436
  133.6 34.2 %copy-start.9 = (bf16[1536,192]{0,1:T(8,128)(2,1)S(1)}, bf16[1536,192]{0,1:T(8,128)(2,1)}, u32[]{:S(2)}) copy-start(bf16[1536,192]{0,1:T(8,128)(2,1)} %param.21) | copy-start | bytes 1769476
  133.6 34.2 %copy-start.11 = (f32[1536]{0:T(1024)S(1)}, f32[1536]{0:T(1024)}, u32[]{:S(2)}) copy-start(f32[1536]{0:T(1024)} %param.20) | copy-start | bytes 18436
  133.6 34.2 %copy-start.13 = (f32[192]{0:T(256)S(1)}, f32[192]{0:T(256)}, u32[]{:S(2)}) copy-start(f32[192]{0:T(256)} %param.22) | copy-start | bytes 2308
  133.6 34.7 %copy-start.10 = (bf16[254,192]{0,1:T(8,128)(2,1)S(1)}, bf16[254,192]{0,1:T(8,128)(2,1)}, u32[]{:S(2)}) copy-start(bf16[254,192]{0,1:T(8,128)(2,1)} %param.23) | copy-start | bytes 292612
  134.2 52.4 %copy-start.12 = (f32[768]{0:T(1024)S(1)}, f32[768]{0:T(1024)}, u32[]{:S(2)}) copy-start(f32[768]{0:T(1024)} %param.26) | copy-start | bytes 9220
  148.5 8.8 %all-to-all-start = ((f32[4,2,384]{2,1,0:T(2,128)}), f32[4,2,384]{2,1,0:T(2,128)S(1)}, u32[]{:S(2)}, u32[]{:S(2)}) async-start(f32[4,2,384]{2,1,0:T(2,128)} %all_to_all.22), calls=%async_computation | async-start | bytes 24576 | tf_op jit(solution)/shard_map/all_to_all | solution.py:107
  169.3 9.4 %all-to-all-start.1 = ((bf16[4,64,192]{2,1,0:T(8,128)(2,1)}), bf16[4,64,192]{2,1,0:T(8,128)(2,1)S(1)}, u32[]{:S(2)}, u32[]{:S(2)}) async-start(bf16[4,64,192]{2,1,0:T(8,128)(2,1)} %bitcast.8), calls=%async_computation.1 | async-start | bytes 262144 | tf_op jit(solution)/shard_map/all_to_all | solution.py:131
  172.6 100.4 %reduce-scatter.2.cloned.1.call-start = ((), (), s32[]{:S(2)}) async-start(), calls=%async_computation.4 | async-start | bytes 983040 | tf_op jit(solution)/shard_map/reduce_scatter | solution.py:227
  187.2 16.6 %copy-start.2 = (bf16[3,256,192]{1,2,0:T(8,128)(2,1)}, bf16[3,256,192]{1,2,0:T(8,128)(2,1)S(1)}, u32[]{:S(2)}) copy-start(bf16[3,256,192]{1,2,0:T(8,128)(2,1)S(1)} %convert_bitcast_fusion) | copy-start | bytes 884740
  219.6 7.7 %collective-permute-start = (bf16[2,256,192]{1,2,0:T(8,128)(2,1)S(1)}, bf16[2,256,192]{1,2,0:T(8,128)(2,1)S(1)}, u32[]{:S(2)}, u32[]{:S(2)}) collective-permute-start(bf16[2,256,192]{1,2,0:T(8,128)(2,1)S(1)} %slice.71), channel_id=1, source_target_pairs={{0,4},{4,0},{8,12},{12,8},{1,5},{5,1},{9,13},{13,9},{2,6},{6,2},{1... | collective-permute-start | bytes 589832 | tf_op jit(solution)/shard_map/ppermute | solution.py:20
  220.5 19.7 %slice-start = ((bf16[3,256,192]{1,2,0:T(8,128)(2,1)}), bf16[1,256,192]{1,2,0:T(8,128)(2,1)S(1)}, s32[]{:S(2)}) async-start(bf16[3,256,192]{1,2,0:T(8,128)(2,1)} %copy-done.2), calls=%async_computation.5 | async-start | bytes 196608 | tf_op jit(solution)/shard_map/slice | solution.py:163
  227.3 12.5 %collective-permute-start.1 = (bf16[2,512,192]{1,2,0:T(8,128)(2,1)S(1)}, bf16[2,512,192]{1,2,0:T(8,128)(2,1)S(1)}, u32[]{:S(2)}, u32[]{:S(2)}) collective-permute-start(bf16[2,512,192]{1,2,0:T(8,128)(2,1)S(1)} %maximum_select_fusion.1), channel_id=1, source_target_pairs={{0,8},{4,12},{8,0},{12,4},{1,9},{5,13},{9,1},{13,5},{2,10},{6,14},... | collective-permute-start | bytes 1179656 | tf_op jit(solution)/shard_map/ppermute | solution.py:20
  242.1 7.2 %copy-start.8 = (f32[192]{0:T(256)S(1)}, f32[192]{0:T(256)}, u32[]{:S(2)}) copy-start(f32[192]{0:T(256)} %param.28) | copy-start | bytes 2308
  242.1 7.3 %copy-start.4 = (bf16[192,768]{1,0:T(8,128)(2,1)S(1)}, bf16[192,768]{1,0:T(8,128)(2,1)}, u32[]{:S(2)}) copy-start(bf16[192,768]{1,0:T(8,128)(2,1)} %param.29) | copy-start | bytes 884740
Sparse Core Ops, SparseCore 0:
  8.9 118.0 all-gather.2
  250.7 22.2 reduce-scatter.1
where the time goes:
time: 282 us; the launch traced here: 281 us
  waiting for transfers between devices  161 us (57%)
  blocking collectives  62.7 us (22%)
  between operations  14.7 us (5%)
  local copies, waits for them, and re-layouts  12.1 us (4%)
  matrix products  11.7 us (4%)
  other arithmetic  11.2 us (4%)
  starting transfers between devices  7.51 us (3%)
    all_gather x1, waiting for transfers between devices, body(): lax.all_gather(w_gate_up, 'seq', axis=1, tiled=True)  110 us
    reduce_scatter x1, waiting for transfers between devices, body(): lax.psum_scatter(partial_rows, 'head', scatter_dimension=1, tiled=True)  22.4 us
    ppermute x2, waiting for transfers between devices, from_partner(): return lax.ppermute(value, axis, pairs)  17.9 us
    all_gather x1, blocking collectives, body(): every_row = lax.all_gather(middle_key_value, 'seq', axis=1, tiled=True)  14 us
    all_gather x1, blocking collectives, body(): lax.all_gather(distant_local_rows[1:], 'seq', axis=1, tiled=True)  13.3 us
    all_gather x1, blocking collectives, body(): everyone = lax.all_gather(pooled_hidden, 'seq', axis=0, tiled=True)  13.2 us
    psum x1, blocking collectives, body(): summed = lax.psum(pooled_part, 'head')  10.1 us
    all_gather x1, blocking collectives, body(): sequence = lax.all_gather(own_part, 'head', axis=1, tiled=True)  6.37 us
  transfers between devices with their start and end apart: 6, of which 6 were waited for; matrix products, arithmetic and copies ran while one was open for 4% of the time, Pallas kernels for 0%

commit v1 on v0

--- a/solution.py
+++ b/solution.py
@@ -12,6 +12,22 @@
 DILATION_THIRD = 16
 layer_eps = 1e-05
 masked_score = -1e30
+
+
+def summed_both_ways(x, axis, dim, term):
+    devices, index, width = (lax.axis_size(axis), lax.axis_index(axis), x.shape[dim])
+    upward = [(i, (i + 1) % devices) for i in range(devices)]
+    left = [(i, (i - 1) % devices) for i in range(devices)]
+    middle = devices // 2
+    from_left = from_right = x
+    total = term(x, index * width)
+    for step in range(1, middle + 1):
+        from_left = lax.ppermute(from_left, axis, upward)
+        if step < devices - middle:
+            from_right = lax.ppermute(from_right, axis, left)
+            total = total + term(from_right, (index + step) % devices * width)
+        total = total + term(from_left, (index - step) % devices * width)
+    return total
 
 
 def from_partner(value, axis, bit):
@@ -92,11 +108,16 @@
     token_rows = tile_tokens.reshape(new_count * patch_count, tile_width)
     normed = normalize(token_rows.astype(jnp.float32), tile_gain).astype(jnp.bfloat16)
     hidden_width = w_gate_up.shape[2]
-    gate_up = jnp.einsum(
-        "rk,gkf->grf",
-        normed,
-        lax.all_gather(w_gate_up, "seq", axis=1, tiled=True),
-        preferred_element_type=jnp.float32,
+    gate_up = summed_both_ways(
+        w_gate_up,
+        "seq",
+        1,
+        lambda own_block, at: jnp.einsum(
+            "rk,gkf->grf",
+            lax.dynamic_slice_in_dim(normed, at, own_block.shape[1], axis=1),
+            own_block,
+            preferred_element_type=jnp.float32,
+        ),
     )
     hidden = (jax.nn.silu(gate_up[0]) * gate_up[1]).astype(jnp.bfloat16)
     pooled_hidden = jnp.mean(

time: 282 us -> 265 us (0.940)
  waiting for transfers between devices: 161 us -> 135 us
  starting transfers between devices: 7.51 us -> 12.9 us
    all_gather x1 -> x0, waiting for transfers between devices: 110 us -> none  [body(): lax.all_gather(w_gate_up, 'seq', axis=1, tiled=True)]
    ppermute x0 -> x3, waiting for transfers between devices: none -> 83.7 us  [the longest x2 55.7 us: summed_both_ways(): from_left = lax.ppermute(from_left, axis, upward)]
    ppermute x0 -> x3, starting transfers between devices: none -> 5.14 us  [the longest x2 3.05 us: summed_both_ways(): from_left = lax.ppermute(from_left, axis, upward)]
    dot_general x1 -> x4, matrix products: 5.96 us -> 8.01 us  [body(): jnp.einsum('rk,gkf->grf', lax.dynamic_slice_in_dim(normed, at, own_block....]
  transfers between devices with their start and end apart: 6 -> 8, of which waited for: 6 -> 8; matrix products, arithmetic and copies ran while one was open for 4% -> 7% of each run, Pallas kernels for 0% -> 0%
where the time goes in v1:
time: 265 us; the launch traced here: 264 us
  waiting for transfers between devices  135 us (51%)
  blocking collectives  63 us (24%)
  between operations  14.8 us (6%)
  matrix products  13.7 us (5%)
  starting transfers between devices  12.9 us (5%)
  other arithmetic  12.9 us (5%)
  local copies, waits for them, and re-layouts  12.1 us (5%)
    ppermute x2, waiting for transfers between devices, summed_both_ways(): from_left = lax.ppermute(from_left, axis, upward)  55.7 us
    ppermute x1, waiting for transfers between devices, summed_both_ways(): from_right = lax.ppermute(from_right, axis, left)  28 us
    reduce_scatter x1, waiting for transfers between devices, body(): lax.psum_scatter(partial_rows, 'head', scatter_dimension=1, tiled=True)  22.8 us
    ppermute x2, waiting for transfers between devices, from_partner(): return lax.ppermute(value, axis, pairs)  17.7 us
    all_gather x1, blocking collectives, body(): every_row = lax.all_gather(middle_key_value, 'seq', axis=1, tiled=True)  14.4 us
    all_gather x1, blocking collectives, body(): everyone = lax.all_gather(pooled_hidden, 'seq', axis=0, tiled=True)  13.2 us
    all_gather x1, blocking collectives, body(): lax.all_gather(distant_local_rows[1:], 'seq', axis=1, tiled=True)  13.1 us
    psum x1, blocking collectives, body(): summed = lax.psum(pooled_part, 'head')  10.1 us
  transfers between devices with their start and end apart: 8, of which 8 were waited for; matrix products, arithmetic and copies ran while one was open for 7% of the time, Pallas kernels for 0%

profile of v1, /device:TPU:0, one launch (start us, length us, event | category | flops | bytes accessed | tf_op | source)
XLA Modules:
  0.0 264.3 jit_solution(5176897160075647201)
XLA Ops:
  6.5 3.1 %collective-permute-start.1 = (bf16[2,384,1024]{2,1,0:T(8,128)(2,1)}, bf16[2,384,1024]{2,1,0:T(8,128)(2,1)}, u32[]{:S(2)}, u32[]{:S(2)}) collective-permute-start(bf16[2,384,1024]{2,1,0:T(8,128)(2,1)} %param.17), channel_id=1, source_target_pairs={{0,4},{4,8},{8,12},{12,0},{1,5},{5,9},{9,13},{13,1},{2,6},{6,10},{... | collective-permute-start | bytes 4718600 | tf_op jit(solution)/shard_map/ppermute | solution.py:25
  9.6 2.1 collective-permute-start
  12.4 0.7 compare_select_fusion
  13.1 2.0 convert_reduce_fusion.1
  15.1 4.3 %scatter_custom_fusion = s32[1024]{0:T(1024)S(1)} fusion(s32[1024]{0:T(1024)S(1)} %compare_select_fusion, s32[1024]{0:T(1024)S(1)} %iota.73, s32[]{:T(128)} %constant.167.clone.1), kind=kCustom, calls=%fused_computation.113 | custom fusion | bytes 4100 | tf_op jit(solution)/shard_map/scatter | solution.py:144
  19.4 0.8 and_select_fusion.2
  20.2 0.2 convert_reduce_fusion.4
  20.5 2.0 multiply_reduce_fusion
  22.5 0.2 convert_reduce_fusion.5
  22.8 24.4 %collective-permute-done.1 = bf16[2,384,1024]{2,1,0:T(8,128)(2,1)} collective-permute-done((bf16[2,384,1024]{2,1,0:T(8,128)(2,1)}, bf16[2,384,1024]{2,1,0:T(8,128)(2,1)}, u32[]{:S(2)}, u32[]{:S(2)}) %collective-permute-start.1) | collective-permute-done | bytes 1572896 | tf_op jit(solution)/shard_map/ppermute | solution.py:25
  47.2 0.5 fusion.4
  47.8 1.3 fusion.23
  49.1 2.7 %fusion.19 = f32[512,2,1024]{2,0,1:T(8,128)S(1)} fusion(bf16[2,384,1024]{2,1,0:T(8,128)(2,1)} %collective-permute-done.1, bf16[512,1536]{1,0:T(8,128)(2,1)S(1)} %fusion.4, s32[]{:T(128)S(6)} %select_n.209), kind=kOutput, calls=%fused_computation.43 | convolution fusion | flops 805306368 | bytes 6160388 | tf_op jit(solution)/shard_map/rk,gkf->grf/dot_general | solution.py:115
  51.7 28.0 %collective-permute-done = bf16[2,384,1024]{2,1,0:T(8,128)(2,1)} collective-permute-done((bf16[2,384,1024]{2,1,0:T(8,128)(2,1)}, bf16[2,384,1024]{2,1,0:T(8,128)(2,1)}, u32[]{:S(2)}, u32[]{:S(2)}) %collective-permute-start) | collective-permute-done | bytes 1572896 | tf_op jit(solution)/shard_map/ppermute | solution.py:27
  79.7 2.7 %fusion.21 = f32[512,2,1024]{2,0,1:T(8,128)S(1)} fusion(bf16[2,384,1024]{2,1,0:T(8,128)(2,1)} %collective-permute-done, bf16[512,1536]{1,0:T(8,128)(2,1)S(1)} %fusion.4, s32[]{:T(128)S(6)} %select_n.207), kind=kOutput, calls=%fused_computation.45 | convolution fusion | flops 805306368 | bytes 6160388 | tf_op jit(solution)/shard_map/rk,gkf->grf/dot_general | solution.py:115
  82.4 31.3 %collective-permute-done.2 = bf16[2,384,1024]{2,1,0:T(8,128)(2,1)S(1)} collective-permute-done((bf16[2,384,1024]{2,1,0:T(8,128)(2,1)}, bf16[2,384,1024]{2,1,0:T(8,128)(2,1)S(1)}, u32[]{:S(2)}, u32[]{:S(2)}) %collective-permute-start.2) | collective-permute-done | bytes 1572896 | tf_op jit(solution)/shard_map/ppermute | solution.py:25
  113.7 1.4 add_bitcast_fusion
  115.1 0.5 fusion.65
  115.7 0.6 convert_reduce_fusion.2
  116.3 13.2 %all-gather = f32[4,2,1024]{2,1,0:T(2,128)S(1)} all-gather(f32[1,2,1024]{2,1,0:T(2,128)S(1)} %multiply_bitcast_fusion), channel_id=1, replica_groups=mesh['groups'=2,'seq'=4,'head'=4] {'seq'}, dimensions={0}, use_global_device_ids=true | all-gather | bytes 40960 | tf_op jit(solution)/shard_map/all_gather | solution.py:126
  129.5 0.4 fusion.71
  129.9 0.6 all_to_all.22
  130.5 3.3 %all-to-all-start = ((f32[4,2,384]{2,1,0:T(2,128)}), f32[4,2,384]{2,1,0:T(2,128)S(1)}, u32[]{:S(2)}, u32[]{:S(2)}) async-start(f32[4,2,384]{2,1,0:T(2,128)} %all_to_all.22), calls=%async_computation | async-start | bytes 24576 | tf_op jit(solution)/shard_map/all_to_all | solution.py:128
  133.8 5.6 %all-to-all-done = f32[4,2,384]{2,1,0:T(2,128)S(1)} async-done(((f32[4,2,384]{2,1,0:T(2,128)}), f32[4,2,384]{2,1,0:T(2,128)S(1)}, u32[]{:S(2)}, u32[]{:S(2)}) %all-to-all-start) | async-done | bytes 12320 | tf_op jit(solution)/shard_map/all_to_all | solution.py:128
  139.4 10.1 %psum.21 = f32[2,1536]{1,0:T(2,128)S(1)} all-reduce(f32[2,1536]{1,0:T(2,128)S(1)} %bitcast.147), channel_id=1, replica_groups=mesh['groups'=2,'seq'=4,'head'=4] {'head'}, use_global_device_ids=true, to_apply=%region_7.8 | all-reduce | flops 3072 | bytes 24576 | tf_op jit(solution)/shard_map/psum | solution.py:129
  149.6 0.2 multiply_reduce_fusion.2
  149.9 0.3 fusion.9
  150.1 0.2 copy.70
  150.3 0.2 convolution_convert_fusion
  150.6 0.8 copy.71
  151.3 3.3 %all-to-all-start.1 = ((bf16[4,64,192]{2,1,0:T(8,128)(2,1)}), bf16[4,64,192]{2,1,0:T(8,128)(2,1)S(1)}, u32[]{:S(2)}, u32[]{:S(2)}) async-start(bf16[4,64,192]{2,1,0:T(8,128)(2,1)} %bitcast.11), calls=%async_computation.1 | async-start | bytes 262144 | tf_op jit(solution)/shard_map/all_to_all | solution.py:152
  155.5 5.2 %all-to-all-done.1 = bf16[4,64,192]{2,1,0:T(8,128)(2,1)S(1)} async-done(((bf16[4,64,192]{2,1,0:T(8,128)(2,1)}), bf16[4,64,192]{2,1,0:T(8,128)(2,1)S(1)}, u32[]{:S(2)}, u32[]{:S(2)}) %all-to-all-start.1) | async-done | bytes 98336 | tf_op jit(solution)/shard_map/all_to_all | solution.py:152
  160.7 1.2 gather_fusion
  162.0 6.5 %all_gather.13 = bf16[256,768]{0,1:T(8,128)(2,1)S(1)} all-gather(bf16[256,192]{0,1:T(8,128)(2,1)S(1)} %broadcast_select_fusion.2), channel_id=1, replica_groups=mesh['groups'=2,'seq'=4,'head'=4] {'head'}, dimensions={1}, use_global_device_ids=true | all-gather | bytes 491520 | tf_op jit(solution)/shard_map/all_gather | solution.py:158
  168.6 0.2 fusion.12
  168.8 0.5 fusion.16
  169.4 0.2 copy.76
  169.6 0.4 reshape.505
  170.0 0.6 select_reduce_fusion
  170.8 13.1 %all_gather.15 = bf16[2,64,192]{2,1,0:T(8,128)(2,1)S(1)} all-gather(bf16[2,16,192]{2,1,0:T(8,128)(2,1)S(1)} %slice.61), channel_id=1, replica_groups=mesh['groups'=2,'seq'=4,'head'=4] {'seq'}, dimensions={1}, use_global_device_ids=true | all-gather | bytes 61440 | tf_op jit(solution)/shard_map/all_gather | solution.py:215
  184.0 0.2 fusion.69
  184.2 0.2 fusion.43
  184.7 0.4 reshape.504
  185.1 0.7 select_reduce_fusion.1
  186.2 14.4 %all_gather.14 = bf16[2,256,192]{2,0,1:T(2,128)(2,1)S(1)} all-gather(bf16[2,64,192]{2,0,1:T(2,128)(2,1)S(1)} %copy.79), channel_id=1, replica_groups=mesh['groups'=2,'seq'=4,'head'=4] {'seq'}, dimensions={1}, use_global_device_ids=true | all-gather | bytes 245760 | tf_op jit(solution)/shard_map/all_gather | solution.py:191
  200.6 0.4 fusion.67
  201.2 0.3 fusion.70
  201.5 0.2 fusion.33
  202.2 0.2 convolution_bitcast_fusion.1
  202.4 0.2 copy.84
  202.6 0.3 convolution_bitcast_fusion
  203.1 0.2 copy.86
  203.3 0.2 copy.88
  203.5 6.1 %collective-permute-done.3 = bf16[2,256,192]{1,2,0:T(8,128)(2,1)S(1)} collective-permute-done((bf16[2,256,192]{1,2,0:T(8,128)(2,1)S(1)}, bf16[2,256,192]{1,2,0:T(8,128)(2,1)S(1)}, u32[]{:S(2)}, u32[]{:S(2)}) %collective-permute-start.3) | collective-permute-done | bytes 196640 | tf_op jit(solution)/shard_map/ppermute | solution.py:36
  209.7 1.1 collective-permute-start.4
  210.8 11.6 %collective-permute-done.4 = bf16[2,512,192]{1,2,0:T(8,128)(2,1)S(1)} collective-permute-done((bf16[2,512,192]{1,2,0:T(8,128)(2,1)S(1)}, bf16[2,512,192]{1,2,0:T(8,128)(2,1)S(1)}, u32[]{:S(2)}, u32[]{:S(2)}) %collective-permute-start.4) | collective-permute-done | bytes 393248 | tf_op jit(solution)/shard_map/ppermute | solution.py:36
  222.4 0.2 maximum_select_fusion
  222.6 0.9 fusion
  223.5 1.0 fusion.1
  224.6 1.2 fusion.7
  226.0 5.7 %all-reduce = (f32[256]{0:T(256)S(1)}, f32[256]{0:T(256)S(1)}) all-reduce(f32[256]{0:T(256)S(1)} %get-tuple-element.8, f32[256]{0:T(256)S(1)} %get-tuple-element.7), channel_id=1, replica_groups=mesh['groups'=2,'seq'=4,'head'=4] {'head'}, use_global_device_ids=true, to_apply=%region_25.26 | all-reduce | flops 512 | bytes 4096 | tf_op jit(solution)/shard_map/psum | solution.py:240
  231.8 1.2 fusion.72
  233.1 22.8 %reduce-scatter.2.cloned.1.call-done = f32[256,192]{0,1:T(8,128)} async-done(((f32[256,768]{0,1:T(8,128)}), f32[256,192]{0,1:T(8,128)}) %reduce-scatter.2.cloned.1.call-update) | async-done | bytes 196624 | tf_op jit(solution)/shard_map/reduce_scatter | solution.py:248
  255.8 1.6 convert_add_fusion
  (109 shorter events, 3.9 us)
Async XLA Ops:
  6.5 162.3 %copy-start = (bf16[3,768,192]{1,2,0:T(8,128)(2,1)S(1)}, bf16[3,768,192]{1,2,0:T(8,128)(2,1)}, u32[]{:S(2)}) copy-start(bf16[3,768,192]{1,2,0:T(8,128)(2,1)} %param.27) | copy-start | bytes 2654212
  6.5 40.7 %copy-start.1 = (bf16[2,256,1536]{2,1,0:T(8,128)(2,1)S(1)}, bf16[2,256,1536]{2,1,0:T(8,128)(2,1)}, u32[]{:S(2)}) copy-start(bf16[2,256,1536]{2,1,0:T(8,128)(2,1)} %param.15) | copy-start | bytes 4718596
  6.5 40.7 %copy-start.6 = (f32[1536]{0:T(1024)S(1)}, f32[1536]{0:T(1024)}, u32[]{:S(2)}) copy-start(f32[1536]{0:T(1024)} %param.16) | copy-start | bytes 18436
  6.5 40.7 %collective-permute-start.1 = (bf16[2,384,1024]{2,1,0:T(8,128)(2,1)}, bf16[2,384,1024]{2,1,0:T(8,128)(2,1)}, u32[]{:S(2)}, u32[]{:S(2)}) collective-permute-start(bf16[2,384,1024]{2,1,0:T(8,128)(2,1)} %param.17), channel_id=1, source_target_pairs={{0,4},{4,8},{8,12},{12,0},{1,5},{5,9},{9,13},{13,1},{2,6},{6,10},{... | collective-permute-start | bytes 4718600 | tf_op jit(solution)/shard_map/ppermute | solution.py:25
  9.6 70.1 %collective-permute-start = (bf16[2,384,1024]{2,1,0:T(8,128)(2,1)}, bf16[2,384,1024]{2,1,0:T(8,128)(2,1)}, u32[]{:S(2)}, u32[]{:S(2)}) collective-permute-start(bf16[2,384,1024]{2,1,0:T(8,128)(2,1)} %param.17), channel_id=1, source_target_pairs={{0,12},{4,0},{8,4},{12,8},{1,13},{5,1},{9,5},{13,9},{2,14},{6,2},{... | collective-permute-start | bytes 4718600 | tf_op jit(solution)/shard_map/ppermute | solution.py:27
  22.8 25.0 %copy-start.3 = (bf16[2,384,1024]{2,1,0:T(8,128)(2,1)S(1)}, bf16[2,384,1024]{2,1,0:T(8,128)(2,1)}, u32[]{:S(2)}) copy-start(bf16[2,384,1024]{2,1,0:T(8,128)(2,1)} %param.17) | copy-start | bytes 4718596
  47.2 66.5 %collective-permute-start.2 = (bf16[2,384,1024]{2,1,0:T(8,128)(2,1)}, bf16[2,384,1024]{2,1,0:T(8,128)(2,1)S(1)}, u32[]{:S(2)}, u32[]{:S(2)}) collective-permute-start(bf16[2,384,1024]{2,1,0:T(8,128)(2,1)} %collective-permute-done.1), channel_id=1, source_target_pairs={{0,4},{4,8},{8,12},{12,0},{1,5},{5,9},{9,13},{13,1},{2,6},{6,10},{... | collective-permute-start | bytes 4718600 | tf_op jit(solution)/shard_map/ppermute | solution.py:25
  115.6 13.9 %copy-start.4 = (bf16[1024,384]{1,0:T(8,128)(2,1)S(1)}, bf16[1024,384]{1,0:T(8,128)(2,1)}, u32[]{:S(2)}) copy-start(bf16[1024,384]{1,0:T(8,128)(2,1)} %param.18) | copy-start | bytes 2359300
  115.6 33.9 %copy-start.7 = (f32[1536]{0:T(1024)S(1)}, f32[1536]{0:T(1024)}, u32[]{:S(2)}) copy-start(f32[1536]{0:T(1024)} %param.19) | copy-start | bytes 18436
  115.6 34.2 %copy-start.9 = (bf16[1536,192]{0,1:T(8,128)(2,1)S(1)}, bf16[1536,192]{0,1:T(8,128)(2,1)}, u32[]{:S(2)}) copy-start(bf16[1536,192]{0,1:T(8,128)(2,1)} %param.21) | copy-start | bytes 1769476
  115.7 34.2 %copy-start.11 = (f32[1536]{0:T(1024)S(1)}, f32[1536]{0:T(1024)}, u32[]{:S(2)}) copy-start(f32[1536]{0:T(1024)} %param.20) | copy-start | bytes 18436
  115.7 34.2 %copy-start.13 = (f32[192]{0:T(256)S(1)}, f32[192]{0:T(256)}, u32[]{:S(2)}) copy-start(f32[192]{0:T(256)} %param.22) | copy-start | bytes 2308
  115.7 34.6 %copy-start.10 = (bf16[254,192]{0,1:T(8,128)(2,1)S(1)}, bf16[254,192]{0,1:T(8,128)(2,1)}, u32[]{:S(2)}) copy-start(bf16[254,192]{0,1:T(8,128)(2,1)} %param.23) | copy-start | bytes 292612
  116.3 52.5 %copy-start.12 = (f32[768]{0:T(1024)S(1)}, f32[768]{0:T(1024)}, u32[]{:S(2)}) copy-start(f32[768]{0:T(1024)} %param.26) | copy-start | bytes 9220
  130.5 8.8 %all-to-all-start = ((f32[4,2,384]{2,1,0:T(2,128)}), f32[4,2,384]{2,1,0:T(2,128)S(1)}, u32[]{:S(2)}, u32[]{:S(2)}) async-start(f32[4,2,384]{2,1,0:T(2,128)} %all_to_all.22), calls=%async_computation | async-start | bytes 24576 | tf_op jit(solution)/shard_map/all_to_all | solution.py:128
  151.3 9.4 %all-to-all-start.1 = ((bf16[4,64,192]{2,1,0:T(8,128)(2,1)}), bf16[4,64,192]{2,1,0:T(8,128)(2,1)S(1)}, u32[]{:S(2)}, u32[]{:S(2)}) async-start(bf16[4,64,192]{2,1,0:T(8,128)(2,1)} %bitcast.11), calls=%async_computation.1 | async-start | bytes 262144 | tf_op jit(solution)/shard_map/all_to_all | solution.py:152
  154.7 101.2 %reduce-scatter.2.cloned.1.call-start = ((), (), s32[]{:S(2)}) async-start(), calls=%async_computation.3 | async-start | bytes 983040 | tf_op jit(solution)/shard_map/reduce_scatter | solution.py:248
  169.4 16.4 %copy-start.2 = (bf16[3,256,192]{1,2,0:T(8,128)(2,1)}, bf16[3,256,192]{1,2,0:T(8,128)(2,1)S(1)}, u32[]{:S(2)}) copy-start(bf16[3,256,192]{1,2,0:T(8,128)(2,1)S(1)} %convert_bitcast_fusion) | copy-start | bytes 884740
  202.0 7.6 %collective-permute-start.3 = (bf16[2,256,192]{1,2,0:T(8,128)(2,1)S(1)}, bf16[2,256,192]{1,2,0:T(8,128)(2,1)S(1)}, u32[]{:S(2)}, u32[]{:S(2)}) collective-permute-start(bf16[2,256,192]{1,2,0:T(8,128)(2,1)S(1)} %slice.71), channel_id=1, source_target_pairs={{0,4},{4,0},{8,12},{12,8},{1,5},{5,1},{9,13},{13,9},{2,6},{6,2},{1... | collective-permute-start | bytes 589832 | tf_op jit(solution)/shard_map/ppermute | solution.py:36
  203.3 19.4 %slice-start = ((bf16[3,256,192]{1,2,0:T(8,128)(2,1)}), bf16[1,256,192]{1,2,0:T(8,128)(2,1)S(1)}, s32[]{:S(2)}) async-start(bf16[3,256,192]{1,2,0:T(8,128)(2,1)} %copy-done.2), calls=%async_computation.4 | async-start | bytes 196608 | tf_op jit(solution)/shard_map/slice | solution.py:184
  209.7 12.7 %collective-permute-start.4 = (bf16[2,512,192]{1,2,0:T(8,128)(2,1)S(1)}, bf16[2,512,192]{1,2,0:T(8,128)(2,1)S(1)}, u32[]{:S(2)}, u32[]{:S(2)}) collective-permute-start(bf16[2,512,192]{1,2,0:T(8,128)(2,1)S(1)} %maximum_select_fusion.1), channel_id=1, source_target_pairs={{0,8},{4,12},{8,0},{12,4},{1,9},{5,13},{9,1},{13,5},{2,10},{6,14},... | collective-permute-start | bytes 1179656 | tf_op jit(solution)/shard_map/ppermute | solution.py:36
  224.6 7.2 %copy-start.8 = (f32[192]{0:T(256)S(1)}, f32[192]{0:T(256)}, u32[]{:S(2)}) copy-start(f32[192]{0:T(256)} %param.28) | copy-start | bytes 2308
  224.6 7.3 %copy-start.5 = (bf16[192,768]{1,0:T(8,128)(2,1)S(1)}, bf16[192,768]{1,0:T(8,128)(2,1)}, u32[]{:S(2)}) copy-start(bf16[192,768]{1,0:T(8,128)(2,1)} %param.29) | copy-start | bytes 884740
Sparse Core Ops, SparseCore 0:
  233.2 22.6 reduce-scatter.1
